TPU v7x, 1024 devices: a whole 4x8x16 slice. The times are simulated.
1024 devices in a mesh: expert: 16 (over x, y_hi, core), fsdp: 64 (over y_lo, z).
Axes of the slice: x: 4, y: 8 (y_hi: 2, y_lo: 4; y = y_hi * 4 + y_lo), z: 16, core: 2. Of those that a mesh axis runs over, the one named last changes fastest.
Arguments:
- momentum: float32 [16, 7168, 1024], P(None, ('fsdp', 'expert')), may hold values from -6 to 6
- spectral_sq: float32 [16], P('expert'), may hold values from 10752 to 35840
Outputs:
- update: bfloat16 [16, 7168, 1024], P(None, ('fsdp', 'expert'))
All inputs are finite; a program needn't handle non-finite values.
Results may differ from a plain program's by a relative error of at most 0.0064.
Values may be sent and summed in bfloat16 or wider, within the bound.
A program may use at most 32 MiB of HBM per device.

v0:
```python
import jax
import jax.numpy as jnp
from jax import lax
from jax.sharding import Mesh
from jax.sharding import PartitionSpec as P

C = 7168
FSDP = ("fsdp_0", "fsdp_1")
FSDP_EXPERT = ("fsdp_0", "fsdp_1", "expert")


coef_a = 3.4445
coef_b = -4.775
coef_c = 2.0315


def own_block(blocks, axes, turns):
    dims = [lax.axis_size(a) for a in axes]
    blocks = blocks.reshape(*dims, *blocks.shape[1:])
    blocks = blocks.transpose(*turns, *range(len(axes), blocks.ndim))
    blocks = blocks.reshape(-1, *blocks.shape[len(axes) :])
    for k in turns:
        blocks = lax.psum_scatter(blocks, axes[k], scatter_dimension=0, tiled=True)
    return blocks[0]


def in_blocks(array, dim, length):
    dims = array.shape
    blocks = array.reshape(*dims[:dim], length, dims[dim] // length, *dims[dim + 1 :])
    return jnp.moveaxis(blocks, dim, 0)


def summed_rows(array, axes, turns, dim):
    length = lax.axis_size(axes)
    return own_block(in_blocks(array, dim, length), axes, turns)


def joined_along(blocks, dim):
    dims = list(blocks.shape[1:])
    dims[dim] *= blocks.shape[0]
    return jnp.moveaxis(blocks, 0, dim).reshape(dims)


def stacked_from(array, axes, turns):
    blocks = array
    for k in turns:
        blocks = lax.all_gather(blocks, axes[k])
    done = turns[::-1]
    back = [done.index(k) for k in range(len(axes))]
    blocks = blocks.transpose(*back, *range(len(axes), blocks.ndim))
    return blocks.reshape(-1, *array.shape)


def whole_of(array, axes, turns, dim):
    return joined_along(stacked_from(array, axes, turns), dim)


def transpose_dot(left_side, right_side):
    return lax.dot_general(
        left_side, right_side, (((0,), (0,)), ((), ())), preferred_element_type=jnp.float32
    )


def on_device(momentum, spectral_sq):
    gathered = lax.all_to_all(momentum, "expert", split_axis=0, concat_axis=1, tiled=True)
    scaled = (gathered / jnp.sqrt(spectral_sq)[:, None, None]).astype(jnp.bfloat16)
    own_rows = scaled[0]
    matrix_order = own_rows.shape[1]
    half_order = matrix_order // 2
    partial_value = transpose_dot(own_rows, own_rows)
    row_index = lax.broadcasted_iota(jnp.int32, (half_order, half_order), 0)
    col_index = lax.broadcasted_iota(jnp.int32, (half_order, half_order), 1)
    corner_sum = partial_value[:half_order, half_order:]
    folded = jnp.where(
        col_index >= row_index,
        partial_value[:half_order, :half_order],
        partial_value[half_order:, half_order:],
    )
    diagonal = jnp.diagonal(partial_value[half_order:, half_order:])
    summed, diag_sum = (
        summed_rows(jnp.concatenate([corner_sum, folded], 0), FSDP, (1, 0), 0),
        summed_rows(diagonal, FSDP, (1, 0), 0),
    )
    stacked, diag_all = (
        whole_of(summed.astype(jnp.bfloat16), FSDP, (0, 1), 0),
        whole_of(diag_sum.astype(jnp.bfloat16), FSDP, (0, 1), 0),
    )
    corner = stacked[:half_order]
    packed = stacked[half_order:]
    first_block = jnp.where(col_index >= row_index, packed, packed.T)
    second_block = jnp.where(
        row_index > col_index, packed, jnp.where(row_index < col_index, packed.T, diag_all[None, :])
    )
    top_rows = jnp.concatenate([first_block, corner], 1)
    bottom_rows = jnp.concatenate([corner.T, second_block], 1)
    rounded = jnp.concatenate([top_rows, bottom_rows], 0)
    product = jnp.dot(rounded, rounded, preferred_element_type=jnp.float32)
    polynomial = (coef_b * rounded.astype(jnp.float32) + coef_c * product).astype(jnp.bfloat16)
    update = coef_a * own_rows.astype(jnp.float32) + jnp.dot(
        own_rows, polynomial, preferred_element_type=jnp.float32
    )
    result = (update * jnp.sqrt(jnp.float32(C))).astype(jnp.bfloat16)[None]
    return lax.all_to_all(result, "expert", split_axis=1, concat_axis=0, tiled=True)


def solution(mesh):
    finer = Mesh(mesh.devices.reshape(mesh.shape["expert"], 4, 16), ("expert", "fsdp_0", "fsdp_1"))
    return jax.shard_map(
        on_device,
        mesh=finer,
        in_specs=(P(None, FSDP_EXPERT, None), P("expert")),
        out_specs=P(None, FSDP_EXPERT, None),
        check_vma=False,
    )
```

profile of v0, /device:TPU:1, one launch (start us, length us, event | category | flops | bytes accessed | tf_op | source)
XLA Modules:
  0.0 315.8 jit_solution(14943936536920917045)
XLA Ops:
  6.5 2.1 copy.24
  8.6 17.5 %all-to-all-start = ((f32[16,7,1024]{2,1,0:T(8,128)}), f32[16,7,1024]{2,1,0:T(8,128)S(1)}, u32[]{:S(2)}, u32[]{:S(2)}) async-start(f32[16,7,1024]{2,1,0:T(8,128)} %copy.24), calls=%async_computation | async-start | bytes 1048576 | tf_op jit(solution)/shard_map/all_to_all | solution.py:65
  26.1 0.0 reduce-scatter.3.cloned.1.call-start
  26.8 12.9 %all-to-all-done = f32[16,7,1024]{2,1,0:T(8,128)S(1)} async-done(((f32[16,7,1024]{2,1,0:T(8,128)}), f32[16,7,1024]{2,1,0:T(8,128)S(1)}, u32[]{:S(2)}, u32[]{:S(2)}) %all-to-all-start) | async-done | bytes 458784 | tf_op jit(solution)/shard_map/all_to_all | solution.py:65
  39.8 0.3 fusion.13
  40.0 0.7 convolution_bitcast_fusion
  40.7 0.3 fusion.22
  41.1 0.2 pad_maximum_fusion
  41.3 1.5 copy.27
  42.8 0.0 reduce-scatter.3.cloned.1.call-update
  42.8 0.0 reduce-scatter.5.cloned.1.call-start
  42.8 68.1 %reduce-scatter.3.cloned.1.call-done = f32[4,16,512]{2,1,0:T(8,128)} async-done(((f32[64,16,512]{2,1,0:T(8,128)}), f32[4,16,512]{2,1,0:T(8,128)}) %reduce-scatter.3.cloned.1.call-update) | async-done | bytes 131088 | tf_op jit(solution)/shard_map/reduce_scatter | solution.py:23
  111.0 0.0 reduce-scatter.5.cloned.1.call-update
  111.0 0.0 all-gather.6.cloned.1.call-start
  111.0 41.1 %reduce-scatter.5.cloned.1.call-done = f32[1,16,512]{2,1,0:T(8,128)} async-done(((f32[4,16,512]{2,1,0:T(8,128)}), f32[1,16,512]{2,1,0:T(8,128)}) %reduce-scatter.5.cloned.1.call-update) | async-done | bytes 32784 | tf_op jit(solution)/shard_map/reduce_scatter | solution.py:23
  152.1 0.8 convert_element_type.35
  152.9 11.0 %all_gather.20 = bf16[4,16,512]{2,1,0:T(8,128)(2,1)} all-gather(bf16[1,16,512]{2,1,0:T(8,128)(2,1)S(1)} %convert_element_type.35), channel_id=1, replica_groups=mesh['expert'=16,'fsdp_0'=4,'fsdp_1'=16] {'fsdp_0'}, dimensions={0}, use_global_device_ids=true | all-gather | bytes 81920 | tf_op jit(solution)/shard_map/all_gather | solution.py:47
  163.9 0.0 all-gather.6.cloned.1.call-update
  163.9 1.3 dynamic-slice
  165.2 1.2 dynamic-slice.2
  167.1 4.5 %gather_fusion = f32[512]{0:T(512)S(1)} fusion(f32[512,512]{1,0:T(8,128)S(1)} %get-tuple-element.5, s32[512]{0:T(512)S(1)} %bitcast.39), kind=kCustom, calls=%fused_computation | custom fusion | bytes 8192 | tf_op jit(solution)/shard_map/jit(diagonal)/cond/branch_0_fun/gather | solution.py:79
  171.6 0.1 reshape_reshape.8
  171.7 45.8 %all-reduce = f32[64,8]{1,0:T(8,128)S(1)} all-reduce(f32[64,8]{1,0:T(8,128)S(1)} %bitcast.49), channel_id=6, replica_groups=mesh['expert'=16,'fsdp_0'=4,'fsdp_1'=16] {'fsdp_1'}, use_global_device_ids=true, to_apply=%region_2.3.clone | all-reduce | flops 512 | bytes 4096
  217.5 6.6 %all-reduce.1 = bf16[4,8]{1,0:T(4,128)(2,1)S(1)} all-reduce(f32[4,8]{1,0:T(4,128)S(1)} %constant_dynamic-slice_fusion.1), channel_id=7, replica_groups=mesh['expert'=16,'fsdp_0'=4,'fsdp_1'=16] {'fsdp_0'}, use_global_device_ids=true, to_apply=%region_3.4.clone | all-reduce | flops 32 | bytes 192
  224.2 0.6 fusion.17
  224.7 7.6 %all-gather.2 = bf16[4,1,8]{2,1,0:T(2,128)(2,1)S(1)} all-gather(bf16[1,1,8]{2,1,0:T(2,128)(2,1)S(1)} %fusion.17), channel_id=1, replica_groups=mesh['expert'=16,'fsdp_0'=4,'fsdp_1'=16] {'fsdp_0'}, dimensions={0}, use_global_device_ids=true | all-gather | bytes 80 | tf_op jit(solution)/shard_map/all_gather | solution.py:47
  232.4 0.1 copy.26
  232.5 19.8 %all-gather.3 = bf16[16,4,8]{2,1,0:T(4,128)(2,1)S(1)} all-gather(bf16[1,4,8]{2,1,0:T(4,128)(2,1)S(1)} %bitcast.51), channel_id=3, replica_groups=mesh['expert'=16,'fsdp_0'=4,'fsdp_1'=16] {'fsdp_1'}, dimensions={0}, use_global_device_ids=true | all-gather | bytes 1088 | tf_op jit(solution)/shard_map/all_gather | solution.py:47
  252.3 0.1 broadcast_in_dim.18
  252.4 0.1 convert_element_type.33
  252.5 0.0 all-gather.6.cloned.1.call-done
  252.6 1.3 fusion.23
  253.9 0.2 copy.29
  254.2 0.2 copy.31
  254.4 0.2 fusion.10
  254.6 2.9 fusion.9
  257.4 0.4 copy.44
  257.8 0.5 broadcast.31
  258.3 2.0 reduce.2
  260.3 0.1 reshape.53
  260.4 46.4 %all_to_all.21 = bf16[16,2,3584]{2,1,0:T(2,128)(2,1)S(1)} all-to-all(bf16[16,2,3584]{2,1,0:T(2,128)(2,1)S(1)} %reshape.53), channel_id=1, replica_groups=mesh['expert'=16,'fsdp_0'=4,'fsdp_1'=16] {'expert'}, dimensions={0} | all-to-all | bytes 458752 | tf_op jit(solution)/shard_map/all_to_all | solution.py:103
  306.9 0.2 reshape.54
  307.0 1.3 bitcast_reduce_fusion
  308.3 0.1 all_to_all.8
  308.4 0.8 copy.35
  (7 shorter events, 0.1 us)
Async XLA Ops:
  8.6 31.1 %all-to-all-start = ((f32[16,7,1024]{2,1,0:T(8,128)}), f32[16,7,1024]{2,1,0:T(8,128)S(1)}, u32[]{:S(2)}, u32[]{:S(2)}) async-start(f32[16,7,1024]{2,1,0:T(8,128)} %copy.24), calls=%async_computation | async-start | bytes 1048576 | tf_op jit(solution)/shard_map/all_to_all | solution.py:65
  26.1 84.9 %reduce-scatter.3.cloned.1.call-start = ((), (), s32[]{:S(2)}) async-start(), calls=%async_computation.4 | async-start | bytes 2228224 | tf_op jit(solution)/shard_map/reduce_scatter | solution.py:23
  42.8 109.3 %reduce-scatter.5.cloned.1.call-start = ((), (), s32[]{:S(2)}) async-start(), calls=%async_computation.5 | async-start | bytes 163840 | tf_op jit(solution)/shard_map/reduce_scatter | solution.py:23
  111.0 141.6 %all-gather.6.cloned.1.call-start = ((), (), s32[]{:S(2)}) async-start(), calls=%async_computation.6 | async-start | bytes 1114112 | tf_op jit(solution)/shard_map/all_gather | solution.py:47
Sparse Core Ops, SparseCore 0:
  42.9 67.9 reduce-scatter.2
  114.3 37.7 reduce-scatter.4
  164.0 67.9 all-gather.5
where the time goes:
time: 319 us; the launch traced here: 316 us
  blocking collectives  137 us (43%)
  waiting for transfers between devices  122 us (38%)
  starting transfers between devices  17.6 us (6%)
  local copies, waits for them, and re-layouts  16.8 us (5%)
  between operations  14.6 us (5%)
  other arithmetic  3.66 us (1%)
  matrix products  3.59 us (1%)
    reduce_scatter x2, waiting for transfers between devices, own_block(): blocks = lax.psum_scatter(blocks, axes[k], scatter_dimension=0, tiled=True)  109 us
    unnamed x2, blocking collectives  52.4 us
    all_to_all x1, blocking collectives, on_device(): lax.all_to_all(result, 'expert', split_axis=1, concat_axis=0, tiled=True)  46.4 us
    all_gather x3, blocking collectives, stacked_from(): blocks = lax.all_gather(blocks, axes[k])  38.4 us
    all_to_all x1, starting transfers between devices, on_device(): lax.all_to_all(momentum, 'expert', split_axis=0, concat_axis=1, tiled=True)  17.5 us
    all_to_all x1, waiting for transfers between devices, on_device(): lax.all_to_all(momentum, 'expert', split_axis=0, concat_axis=1, tiled=True)  12.9 us
  transfers between devices with their start and end apart: 4, of which 3 were waited for; matrix products, arithmetic and copies ran while one was open for 3% of the time, Pallas kernels for 0%

commit v1 on v0

v1 whole, which is shorter than its diff:
```python
import jax
import jax.numpy as jnp
from jax import lax
from jax.experimental import pallas as pl
from jax.experimental.pallas import tpu as pltpu
from jax.sharding import Mesh
from jax.sharding import PartitionSpec as P

C = 7168
coef_a = 3.4445
coef_b = -4.775
coef_c = 2.0315

AXES = ("x", "yh", "core", "yl", "z")
MESH = pl.DeviceIdType.MESH
LANES = 128
f32 = jnp.float32
bf16 = jnp.bfloat16


def kernel(
    sizes, m_hbm, s_ref, o_ref,
    m_ref, msend, xin, xe, own, psend, precv, acc, qsend, qrecv,
    stored, gram, poly, zrow, osend, sq,
    m_sem, zs, zr, cs, cr, xs, xr, ys, yr, gys, gyr, gxs, gxr, gcs, gcr, os, orv,
    ss, sr,
):
    nx, ny, nz, nyl = sizes
    nb = 2 * nx
    nd = nb // 2 + 1
    x, yh, c, yl, z = [lax.axis_index(a) for a in AXES]
    y = yh * nyl + yl
    expert = (x * 2 + yh) * 2 + c
    part = ny and LANES // ny

    def to_z(d):
        return {"z": lax.rem(z + d, nz)}

    def to_x(d):
        return {"x": lax.rem(x + d, nx)}

    def to_y(d):
        t = lax.rem(y + d, ny)
        return {"yh": t // nyl, "yl": lax.rem(t, nyl)}

    to_core = {"core": 1 - c}

    def far_first(k, n):
        h = (k + 1) // 2
        return n // 2 + h * (1 - 2 * lax.rem(k, 2))

    load = pltpu.make_async_copy(m_hbm, m_ref, m_sem)
    load.start()

    barrier = pltpu.get_barrier_semaphore()

    def greet(k, carry):
        pl.semaphore_signal(barrier, inc=1, device_id=to_z(far_first(k, nz)), device_id_type=MESH)
        return carry

    lax.fori_loop(0, nz - 1, greet, 0)
    for d in range(1, ny):
        pl.semaphore_signal(barrier, inc=1, device_id=to_y(d), device_id_type=MESH)
    for d in range(1, nx):
        pl.semaphore_signal(barrier, inc=1, device_id=to_x(d), device_id_type=MESH)
    pl.semaphore_signal(barrier, inc=1, device_id=to_core, device_id_type=MESH)

    sq[0] = jnp.full(sq.shape[1:], jnp.where(expert == z, s_ref[0], 0.0), f32)
    load.wait()

    def padded(e):
        rows = m_ref[e]
        return jnp.concatenate([rows, jnp.zeros((1, rows.shape[1]), f32)], 0).astype(bf16)

    def cast(e, carry):
        msend[e] = padded(e)
        return carry

    lax.fori_loop(0, nz, cast, 0)
    xin[0, 0] = padded(z)

    pl.semaphore_wait(barrier, (nz - 1) + (ny - 1) + (nx - 1) + 1)

    def remote(src, dst, send_sem, recv_sem, where):
        return pltpu.make_async_remote_copy(
            src_ref=src, dst_ref=dst, send_sem=send_sem, recv_sem=recv_sem,
            device_id=where, device_id_type=MESH,
        )

    def z_copy(d):
        return remote(
            msend.at[lax.rem(z + d, nz)], xin.at[0, d], zs.at[d], zr.at[d], to_z(d)
        )

    def swap_copy(d):
        return remote(xin.at[0, d], xin.at[1, d], cs.at[d], cr.at[d], to_core)

    def z_start(k, carry):
        z_copy(far_first(k, nz)).start()
        return carry

    lax.fori_loop(0, nz - 1, z_start, 0)
    swap_copy(0).start()
    sq_core = remote(sq.at[0], sq.at[1], ss.at[0], sr.at[0], to_core)
    sq_core.start()

    def z_take(k, carry):
        d = nz - 1 - k
        d = lax.rem(far_first(nz - 2 - k, nz), nz)
        z_copy(d).wait_recv()
        swap_copy(d).start()
        return carry

    lax.fori_loop(0, nz - 1, z_take, 0)

    width = nb * LANES
    extra = (nd - 1) * LANES
    half = nz * 8

    def spread(side, k):
        pair = jnp.concatenate(
            [xin[side, 2 * k].astype(f32), xin[side, 2 * k + 1].astype(f32)], 0
        ).astype(bf16)
        rows = pl.ds(pl.multiple_of(side * half + k * 16, 16), 16)
        xe[rows, :width] = pair
        xe[rows, width:] = pair[:, :extra]

    def spread_own(k, carry):
        spread(0, k)
        return carry

    def spread_other(k, carry):
        spread(1, k)
        return carry

    lax.fori_loop(0, nz // 2, spread_own, 0)

    def swap_take(d, carry):
        swap_copy(d).wait_recv()
        return carry

    lax.fori_loop(0, nz, swap_take, 0)
    lax.fori_loop(0, nz // 2, spread_other, 0)

    sq_core.wait_recv()
    sq[2] = sq[0] + sq[1]

    def x_copy(d):
        return remote(psend.at[d], precv.at[d], xs.at[d], xr.at[d], to_x(d))

    def sq_x(d):
        return remote(sq.at[2], sq.at[2 + d], ss.at[d], sr.at[d], to_x(d))

    def partial_gram(d):
        start = pl.multiple_of((2 * lax.rem(x + d, nx) + c) * LANES, LANES)
        return lax.dot_general(
            xe[:, pl.ds(start, LANES)], xe[:, pl.ds(start, nd * LANES)],
            (((0,), (0,)), ((), ())), preferred_element_type=f32,
        )

    order_x = sorted(range(1, nx), key=lambda d: -min(d, nx - d))
    for d in order_x:
        psend[d] = partial_gram(d).astype(bf16)
        x_copy(d).start()
    for d in order_x:
        sq_x(d).start()
    total = partial_gram(0)
    for d in reversed(order_x):
        x_copy(d).wait_recv()
        total = total + precv[d].astype(f32)
    total = total.reshape(acc.shape)
    acc[...] = total
    qsend[...] = total.astype(bf16)

    def y_copy(d):
        return remote(
            qsend.at[lax.rem(y + d, ny)], qrecv.at[d], ys.at[d], yr.at[d], to_y(d)
        )

    order_y = sorted(range(1, ny), key=lambda d: -min(d, ny - d))
    for d in order_y:
        y_copy(d).start()
    s_sum = sq[2]
    for d in order_x:
        sq_x(d).wait_recv()
        s_sum = s_sum + sq[2 + d]
    sq[nx + 2] = s_sum
    sq_y = remote(sq.at[nx + 2], sq.at[nx + 3], ss.at[nx], sr.at[nx], to_y(ny // 2))
    sq_y.start()

    total = acc[y]
    for d in reversed(order_y):
        y_copy(d).wait_recv()
        total = total + qrecv[d].astype(f32)
    sq_y.wait_recv()
    square = sq[nx + 2] + sq[nx + 3]
    inverse = jnp.concatenate([1.0 / square] * nd, 1)
    inverse = jnp.concatenate([inverse] * (part // 8), 0)
    mine = 2 * x + c
    stored[mine, y] = (total * inverse).astype(bf16)

    def gy_copy(d, slot):
        return remote(stored.at[mine, slot], stored.at[mine, slot], gys.at[d], gyr.at[d], to_y(d))

    for d in order_y:
        gy_copy(d, y).start()
    for d in reversed(order_y):
        gy_copy(d, lax.rem(y + ny - d, ny)).wait_recv()

    def block_of(d):
        return 2 * lax.rem(x + nx - d, nx) + c

    def gx_copy(d, slot):
        return remote(stored.at[slot], stored.at[slot], gxs.at[d], gxr.at[d], to_x(d))

    def gc_copy(d, slot):
        return remote(stored.at[slot], stored.at[slot], gcs.at[d], gcr.at[d], to_core)

    for d in order_x:
        gx_copy(d, mine).start()
    gc_copy(0, mine).start()

    def assemble(i):
        rows = pl.ds(pl.multiple_of(i * LANES, LANES), LANES)
        block = stored[i].reshape(LANES, nd * LANES)
        for d in range(nd):
            t = pl.multiple_of(lax.rem(i + d, nb) * LANES, LANES)
            piece = block[:, d * LANES : (d + 1) * LANES]
            gram[rows, pl.ds(t, LANES)] = piece
            if 0 < d < nd - 1:
                gram[pl.ds(t, LANES), rows] = piece.T

    assemble(mine)

    def other(d):
        return 2 * lax.rem(x + nx - d, nx) + 1 - c

    gc_copy(0, other(0)).wait_recv()
    assemble(other(0))
    for d in reversed(order_x):
        gx_copy(d, block_of(d)).wait_recv()
        gc_copy(d, block_of(d)).start()
        assemble(block_of(d))
    for d in reversed(order_x):
        gc_copy(d, other(d)).wait_recv()
        assemble(other(d))

    tile = 256

    def poly_rows(r, carry):
        rows = pl.ds(pl.multiple_of(r * tile, tile), tile)
        g = gram[rows, :]
        square_rows = jnp.dot(g, gram[...], preferred_element_type=f32)
        poly[rows, :] = (coef_b * g.astype(f32) + coef_c * square_rows).astype(bf16)
        return carry

    lax.fori_loop(0, width // tile, poly_rows, 0)

    mat = xe[:half, :width]
    zrow[...] = coef_a * mat.astype(f32) + jnp.dot(mat, poly[...], preferred_element_type=f32)
    scale = jnp.concatenate([jnp.sqrt(f32(C)) / jnp.sqrt(square)] * nb, 1)

    def out_value(d):
        rows = pl.ds(pl.multiple_of(d * 8, 8), 8)
        return (zrow[rows, :] * scale).astype(bf16)

    def o_copy(d):
        return remote(
            osend.at[d], o_ref.at[z], os.at[d], orv.at[d], {"z": lax.rem(z + nz - d, nz)}
        )

    def o_start(k, carry):
        d = far_first(k, nz)
        osend[d] = out_value(d)
        o_copy(d).start()
        return carry

    lax.fori_loop(0, nz - 1, o_start, 0)
    osend[0] = out_value(0)
    keep = pltpu.make_async_copy(osend.at[0], o_ref.at[z], m_sem)
    keep.start()

    def z_sent(d, carry):
        z_copy(d).wait_send()
        swap_copy(d).wait_send()
        return carry

    lax.fori_loop(1, nz, z_sent, 0)
    swap_copy(0).wait_send()
    sq_core.wait_send()
    sq_y.wait_send()
    for d in order_x:
        x_copy(d).wait_send()
        sq_x(d).wait_send()
        gx_copy(d, mine).wait_send()
        gc_copy(d, block_of(d)).wait_send()
    gc_copy(0, mine).wait_send()
    for d in order_y:
        y_copy(d).wait_send()
        gy_copy(d, y).wait_send()

    def o_take(k, carry):
        d = far_first(nz - 2 - k, nz)
        source = lax.rem(z + d, nz)
        remote(
            osend.at[d], o_ref.at[source], os.at[d], orv.at[d], {"z": lax.rem(z + nz - d, nz)}
        ).wait()
        return carry

    lax.fori_loop(0, nz - 1, o_take, 0)
    keep.wait()


def on_device(sizes, momentum, spectral_sq):
    nx, ny, nz, _ = sizes
    nb = 2 * nx
    nd = nb // 2 + 1
    rows, width = momentum.shape[1:]
    assert momentum.shape[0] == nz and width == nb * LANES and rows == 7
    part = LANES // ny
    sem = pltpu.SemaphoreType.DMA
    vmem = pltpu.VMEM
    out = pl.pallas_call(
        lambda *refs: kernel(sizes, *refs),
        out_shape=jax.ShapeDtypeStruct((nz, 8, width), bf16),
        in_specs=[
            pl.BlockSpec(memory_space=pl.ANY),
            pl.BlockSpec(memory_space=pltpu.SMEM),
        ],
        out_specs=pl.BlockSpec(memory_space=pl.ANY),
        scratch_shapes=[
            vmem(momentum.shape, f32),
            vmem((nz, 8, width), bf16),
            vmem((2, nz, 8, width), bf16),
            vmem((2 * nz * 8, width + (nd - 1) * LANES), bf16),
            vmem((8, LANES), f32),
            vmem((nx, LANES, nd * LANES), bf16),
            vmem((nx, LANES, nd * LANES), bf16),
            vmem((ny, part, nd * LANES), f32),
            vmem((ny, part, nd * LANES), bf16),
            vmem((ny, part, nd * LANES), bf16),
            vmem((nb, ny, part, nd * LANES), bf16),
            vmem((width, width), bf16),
            vmem((width, width), bf16),
            vmem((nz * 8, width), f32),
            vmem((nz, 8, width), bf16),
            vmem((nx + 4, 8, LANES), f32),
            sem(()),
            sem((nz,)), sem((nz,)), sem((nz,)), sem((nz,)),
            sem((nx,)), sem((nx,)), sem((ny,)), sem((ny,)),
            sem((ny,)), sem((ny,)), sem((nx,)), sem((nx,)),
            sem((nx,)), sem((nx,)), sem((nz,)), sem((nz,)),
            sem((nx + 1,)), sem((nx + 1,)),
        ],
        compiler_params=pltpu.CompilerParams(
            collective_id=0, has_side_effects=True, vmem_limit_bytes=48 << 20
        ),
        name="muon_step",
    )(momentum, spectral_sq)
    return out[:, :rows]


def solution(mesh):
    ne, nf = mesh.shape["expert"], mesh.shape["fsdp"]
    nx, nyl = ne // 4, 4
    nz = nf // nyl
    sizes = (nx, 2 * nyl, nz, nyl)
    finer = Mesh(mesh.devices.reshape(nx, 2, 2, nyl, nz), AXES)
    rows = P(None, ("yl", "z", "x", "yh", "core"), None)
    return jax.shard_map(
        lambda m, s: on_device(sizes, m, s),
        mesh=finer,
        in_specs=(rows, P(("x", "yh", "core"))),
        out_specs=rows,
        check_vma=False,
    )
```

time: 319 us -> 92.6 us (0.29)
  blocking collectives: 137 us -> 0 us
  waiting for transfers between devices: 122 us -> 0 us
  Pallas kernels: 0 us -> 89.2 us
  starting transfers between devices: 17.6 us -> 0 us
  local copies, waits for them, and re-layouts: 16.8 us -> 2.13 us
  between operations: 14.6 us -> 0.66 us
  other arithmetic: 3.66 us -> 0 us
  matrix products: 3.59 us -> 0 us
    reduce_scatter x2 -> x0, waiting for transfers between devices: 109 us -> none  [own_block(): blocks = lax.psum_scatter(blocks, axes[k], scatter_dimension=0, tiled=True)]
    pallas_call x0 -> x1, Pallas kernels: none -> 89.2 us  [on_device(): pl.pallas_call(lambda *refs: kernel(sizes, *refs), out_shape=jax.ShapeDty...]
    unnamed x2 -> x0, blocking collectives: 52.4 us -> none
    all_to_all x1 -> x0, blocking collectives: 46.4 us -> none  [on_device(): lax.all_to_all(result, 'expert', split_axis=1, concat_axis=0, tiled=True)]
    all_gather x3 -> x0, blocking collectives: 38.4 us -> none  [stacked_from(): blocks = lax.all_gather(blocks, axes[k])]
    all_to_all x1 -> x0, starting transfers between devices: 17.5 us -> none  [on_device(): lax.all_to_all(momentum, 'expert', split_axis=0, concat_axis=1, tiled=True)]
    all_to_all x1 -> x0, waiting for transfers between devices: 12.9 us -> none  [on_device(): lax.all_to_all(momentum, 'expert', split_axis=0, concat_axis=1, tiled=True)]
    unnamed x9 -> x1, local copies, waits for them, and re-layouts: 6.01 us -> 1.29 us
  transfers between devices with their start and end apart: 4 -> 0, of which waited for: 3 -> 0; matrix products, arithmetic and copies ran while one was open for 3% -> 0% of each run, Pallas kernels for 0% -> 0%
where the time goes in v1:
time: 92.6 us; the launch traced here: 92 us
  Pallas kernels  89.2 us (96%)
  local copies, waits for them, and re-layouts  2.13 us (2%)
    pallas_call x1, Pallas kernels, on_device(): pl.pallas_call(lambda *refs: kernel(sizes, *refs), out_shape=jax.ShapeDty...  89.2 us

profile of v1, /device:TPU:1, one launch (start us, length us, event | category | flops | bytes accessed | tf_op | source)
XLA Modules:
  0.0 92.0 jit_solution(10950422787284801631)
XLA Ops:
  0.7 1.3 %copy.3.refs_0_ = f32[16,7,1024]{2,1,0:T(8,128)S(1)} copy(f32[16,7,1024]{2,0,1:T(8,128)} %param.2) | data formatting | bytes 917504 | tf_op args[0]
  1.9 89.2 %muon_step.1 = bf16[16,8,1024]{2,1,0:T(8,128)(2,1)S(1)} custom-call(f32[16,7,1024]{2,1,0:T(8,128)S(1)} %copy.3.refs_0_, f32[1]{0:T(128)S(6)} %copy.5.refs_1_), custom_call_target="tpu_custom_call" | custom-call | tf_op jit(solution)/shard_map/muon_step/pallas_call | solution.py:323
  91.1 0.8 copy.4

commit v2 on v0

v2 whole, which is shorter than its diff:
```python
import jax
import jax.numpy as jnp
from jax import lax
from jax.experimental import pallas as pl
from jax.experimental.pallas import tpu as pltpu
from jax.sharding import Mesh
from jax.sharding import PartitionSpec as P

C = 7168
coef_a = 3.4445
coef_b = -4.775
coef_c = 2.0315

AXES = ("x", "yh", "core", "yl", "z")
MESH = pl.DeviceIdType.MESH
LANES = 128
ROWS = 7
f32 = jnp.float32
bf16 = jnp.bfloat16

CHUNKS = (1, 2, 3, 4, 0)
STEPS = (
    "X0 X1 X2 Y0 X3 Y1 X4 Y2 A0 Y3 A1 Y4 A2 B0 A3 B1 A4 B2 B3 B4".split()
)
OUT_CUTS = (0, 384, 896)


def row_of(shape):
    return lax.broadcasted_iota(jnp.int32, shape, 0)


def spread_rows(last):
    return jnp.concatenate(
        [jnp.broadcast_to(last[j : j + 1], (8, LANES)) for j in range(ROWS)], 1
    )


def last_block(packed):
    out = jnp.zeros((8, LANES), f32)
    row = row_of(out.shape)
    for j in range(ROWS):
        piece = packed[ROWS : ROWS + 1, j * LANES : (j + 1) * LANES]
        out = jnp.where(row == j, jnp.broadcast_to(piece, out.shape), out)
    return out


def kernel(
    sizes, m_hbm, s_ref, o_ref,
    m_ref, msend, xin, xe, xb, psend, precv, own, acc, qsend, qrecv,
    stored, gram, poly, zrow, tail, osend, orecv, sq,
    m_sem, zs, zr, cs, cr, xs, xr, ys, yr, gys, gyr, gxs, gxr, gcs, gcr, os, orv,
    ss, sr,
):
    nx, ny, nz, nyl = sizes
    nb = 2 * nx
    nd = nb // 2 + 1
    x, yh, c, yl, z = [lax.axis_index(a) for a in AXES]
    y = yh * nyl + yl
    expert = (x * 2 + yh) * 2 + c
    part = LANES // ny
    width = nb * LANES
    short = ROWS * LANES
    half = nz * 8
    order_x = sorted(range(1, nx), key=lambda d: -min(d, nx - d))
    pending = []

    def to_z(d):
        return {"z": lax.rem(z + d, nz)}

    def to_x(d):
        return {"x": lax.rem(x + d, nx)}

    def to_y(d):
        t = lax.rem(y + d, ny)
        return {"yh": t // nyl, "yl": lax.rem(t, nyl)}

    to_core = {"core": 1 - c}

    def mixed(k, n):
        g, r = jnp.maximum(k - 1, 0) // 4, lax.rem(jnp.maximum(k - 1, 0), 4)
        near = 1 + g + lax.rem(r, 2) * (n - 2 - 2 * g)
        far = n // 2 - 1 - g + lax.rem(r, 2) * (2 + 2 * g)
        return jnp.where(k == 0, n // 2, jnp.where(r < 2, near, far))

    def mixed_late(k, n):
        return mixed(lax.rem(k + 1, n - 1), n)

    def each(n, body):
        def step(k, carry):
            body(k)
            return carry

        lax.fori_loop(0, n, step, 0)

    def remote(src, dst, send_sem, recv_sem, where):
        return pltpu.make_async_remote_copy(
            src_ref=src, dst_ref=dst, send_sem=send_sem, recv_sem=recv_sem,
            device_id=where, device_id_type=MESH,
        )

    load = pltpu.make_async_copy(m_hbm, m_ref, m_sem)
    load.start()

    barrier = pltpu.get_barrier_semaphore()

    def greet(where):
        pl.semaphore_signal(barrier, inc=1, device_id=where, device_id_type=MESH)

    each(nz - 1, lambda k: greet(to_z(mixed(k, nz))))
    each(ny - 1, lambda k: greet(to_y(mixed(k, ny))))
    for d in order_x:
        greet(to_x(d))
    greet(to_core)

    sq[0] = jnp.full(sq.shape[1:], jnp.where(expert == z, s_ref[0], 0.0), f32)

    def packed(rows):
        end = jnp.concatenate([rows[j : j + 1, short:] for j in range(ROWS)], 1)
        return jnp.concatenate([rows[:, :short], end], 0).astype(bf16)

    group = min(nz, 8)

    def cast(g):
        first = pl.multiple_of(g * group, group)
        turned = jnp.swapaxes(m_ref[:, pl.ds(first, group), :], 0, 1)
        for i in range(group):
            msend[first + i] = packed(turned[i])

    load.wait()
    each(nz // group, cast)
    xin[0, 0] = msend[z]

    pl.semaphore_wait(barrier, (nz - 1) + (ny - 1) + (nx - 1) + 1)

    def z_copy(d):
        return remote(
            msend.at[lax.rem(z + d, nz)], xin.at[0, d], zs.at[d], zr.at[d], to_z(d)
        )

    def swap_copy(d):
        return remote(xin.at[0, d], xin.at[1, d], cs.at[d], cr.at[d], to_core)

    each(nz - 1, lambda k: z_copy(mixed(k, nz)).start())
    sq_core = remote(sq.at[0], sq.at[1], ss.at[0], sr.at[0], to_core)
    sq_core.start()
    swap_copy(0).start()

    def unpack(side, d):
        rows = pl.ds(pl.multiple_of(side * half + d * 8, 8), 8)
        flat = xin[side, d].astype(f32)
        xe[rows, :short] = jnp.where(row_of(flat.shape) < ROWS, flat, 0.0)
        xe[rows, short:width] = last_block(flat)

    def z_take(k):
        d = mixed_late(k, nz)
        z_copy(d).wait_recv()
        swap_copy(d).start()
        unpack(0, d)

    unpack(0, 0)
    each(nz - 1, z_take)

    def swap_take(d):
        swap_copy(d).wait_recv()
        unpack(1, d)

    swap_take(0)
    each(nz - 1, lambda k: swap_take(mixed_late(k, nz)))
    sq_core.wait_recv()
    sq[2] = sq[0] + sq[1]

    def z_sent(d):
        z_copy(d + 1).wait_send()
        swap_copy(d + 1).wait_send()

    pending.append(lambda: each(nz - 1, z_sent))
    pending.append(swap_copy(0).wait_send)
    pending.append(sq_core.wait_send)

    def sq_x(d):
        return remote(sq.at[2], sq.at[2 + d], ss.at[d], sr.at[d], to_x(d))

    for d in order_x:
        sq_x(d).start()
        pending.append(sq_x(d).wait_send)

    xb[...] = xe[...].astype(bf16)

    def x_copy(j, d):
        return remote(psend.at[j, d], precv.at[j, d], xs.at[j, d], xr.at[j, d], to_x(d))

    def columns(first):
        t = lax.rem(first, nb)
        return xb[:, pl.ds(pl.multiple_of(t * LANES, LANES), LANES)]

    def partial_gram(d):
        first = 2 * lax.rem(x + d, nx) + c
        right = jnp.concatenate([columns(first + j) for j in range(nd)], 1)
        return lax.dot_general(
            columns(first), right, (((0,), (0,)), ((), ())), preferred_element_type=f32
        )

    for d in order_x:
        value = partial_gram(d).astype(bf16)
        for j in range(nd):
            psend[j, d] = value[:, j * LANES : (j + 1) * LANES]
    for j in CHUNKS[:nd]:
        for d in order_x:
            x_copy(j, d).start()
            pending.append(x_copy(j, d).wait_send)
    value = partial_gram(0)
    for j in range(nd):
        own[j] = value[:, j * LANES : (j + 1) * LANES]

    mine = 2 * x + c
    sq_y = remote(sq.at[nx + 2], sq.at[nx + 3], ss.at[nx], sr.at[nx], to_y(ny // 2))
    inverse = []

    def y_copy(j, d):
        return remote(
            qsend.at[j, lax.rem(y + d, ny)], qrecv.at[j, d], ys.at[j, d], yr.at[j, d], to_y(d)
        )

    def gy_copy(j, d, slot):
        return remote(
            stored.at[j, mine, slot], stored.at[j, mine, slot], gys.at[j, d], gyr.at[j, d], to_y(d)
        )

    def gx_copy(j, d, slot):
        return remote(
            stored.at[j, slot], stored.at[j, slot], gxs.at[j, d], gxr.at[j, d], to_x(d)
        )

    def gc_copy(j, d, slot):
        return remote(
            stored.at[j, slot], stored.at[j, slot], gcs.at[j, d], gcr.at[j, d], to_core
        )

    def block_of(d, core):
        return 2 * lax.rem(x + nx - d, nx) + core

    def assemble(j, i):
        rows = pl.ds(pl.multiple_of(i * LANES, LANES), LANES)
        cols = pl.ds(pl.multiple_of(lax.rem(i + j, nb) * LANES, LANES), LANES)
        piece = stored[j, i].reshape(LANES, LANES)
        gram[rows, cols] = piece
        if 0 < j < nd - 1:
            gram[cols, rows] = piece.T

    def step_x(j, first):
        total = own[j]
        for d in reversed(order_x):
            x_copy(j, d).wait_recv()
            total = total + precv[j, d].astype(f32)
        total = total.reshape(acc.shape[1:])
        acc[j] = total
        qsend[j] = total.astype(bf16)
        if first:
            s_sum = sq[2]
            for d in order_x:
                sq_x(d).wait_recv()
                s_sum = s_sum + sq[2 + d]
            sq[nx + 2] = s_sum
            sq_y.start()
            pending.append(sq_y.wait_send)
        each(ny - 1, lambda k: y_copy(j, mixed(k, ny)).start())
        pending.append(lambda: each(ny - 1, lambda k: y_copy(j, k + 1).wait_send()))

    def step_y(j, first):
        if first:
            sq_y.wait_recv()
            square = sq[nx + 2] + sq[nx + 3]
            sq[nx + 4] = square
            inverse.append(jnp.concatenate([1.0 / square] * (part // 8), 0))

        def add(k, total):
            d = mixed_late(k, ny)
            y_copy(j, d).wait_recv()
            return total + qrecv[j, d].astype(f32)

        total = lax.fori_loop(0, ny - 1, add, acc[j, y])
        stored[j, mine, y] = (total * inverse[0]).astype(bf16)
        each(ny - 1, lambda k: gy_copy(j, mixed(k, ny), y).start())
        pending.append(lambda: each(ny - 1, lambda k: gy_copy(j, k + 1, y).wait_send()))

    def step_a(j, first):
        def take(k):
            d = mixed_late(k, ny)
            gy_copy(j, d, lax.rem(y + ny - d, ny)).wait_recv()

        each(ny - 1, take)
        for d in order_x:
            gx_copy(j, d, mine).start()
            pending.append(gx_copy(j, d, mine).wait_send)
        gc_copy(j, 0, mine).start()
        pending.append(gc_copy(j, 0, mine).wait_send)
        assemble(j, mine)

    late = []

    def step_b(j, first):
        for d in reversed(order_x):
            gx_copy(j, d, block_of(d, c)).wait_recv()
            gc_copy(j, d, block_of(d, c)).start()
            pending.append(gc_copy(j, d, block_of(d, c)).wait_send)
            assemble(j, block_of(d, c))
        for k in late:
            others(k)
        late[:] = [j]

    def others(j):
        for d in (0, *reversed(order_x)):
            gc_copy(j, d, block_of(d, 1 - c)).wait_recv()
            assemble(j, block_of(d, 1 - c))

    steps = {"X": step_x, "Y": step_y, "A": step_a, "B": step_b}
    seen = set()
    chunks = [j for j in CHUNKS if j < nd]
    for name in STEPS:
        if int(name[1]) < nd:
            steps[name[0]](chunks[int(name[1])], name[0] not in seen)
            seen.add(name[0])
    for k in late:
        others(k)

    def update_columns(*cuts):
        def joined(ref, rows=slice(None)):
            return jnp.concatenate([ref[rows, cut] for cut in cuts], 1)

        right = joined(gram)
        square_cols = jnp.dot(gram[...], right, preferred_element_type=f32)
        poly[:, : right.shape[1]] = (
            coef_b * right.astype(f32) + coef_c * square_cols
        ).astype(bf16)
        value = coef_a * joined(xe, slice(half)) + jnp.dot(
            xb[:half, :], poly[:, : right.shape[1]], preferred_element_type=f32
        )
        at = 0
        for cut in cuts:
            size = cut.stop - cut.start
            zrow[:, cut] = value[:, at : at + size]
            at += size

    root = jnp.sqrt(f32(C)) / jnp.sqrt(sq[nx + 4])

    def tail_rows(d):
        rows = pl.ds(pl.multiple_of(d * 8, 8), 8)
        tail[rows, :] = spread_rows(zrow[rows, short:] * root)

    def o_copy(q, d, source):
        cols = pl.ds(OUT_CUTS[q], OUT_CUTS[q + 1] - OUT_CUTS[q])
        return remote(
            osend.at[d, :, cols], orecv.at[source, :, cols], os.at[q, d], orv.at[q, d],
            {"z": lax.rem(z + nz - d, nz)},
        )

    def send_back(q, d):
        cols = slice(OUT_CUTS[q], OUT_CUTS[q + 1])
        rows = pl.ds(pl.multiple_of(d * 8, 8), 8)
        scale = jnp.concatenate([root] * ((cols.stop - cols.start) // LANES), 1)
        value = zrow[rows, cols] * scale
        value = jnp.where(row_of(value.shape) < ROWS, value, tail[rows, cols])
        osend[d, :, cols] = value.astype(bf16)

    for q in range(len(OUT_CUTS) - 1):
        cut = slice(OUT_CUTS[q], OUT_CUTS[q + 1])
        if q == 0:
            update_columns(slice(short, width), cut)
            each(nz, tail_rows)
        else:
            update_columns(cut)

        def o_start(k, q=q):
            d = mixed(k, nz)
            send_back(q, d)
            o_copy(q, d, z).start()

        each(nz - 1, o_start)
        send_back(q, 0)

    for wait in pending:
        wait()

    def put(e, value):
        o_ref[e, :, :short] = value
        o_ref[e, :, short:] = last_block(value.astype(f32)).astype(bf16)

    put(z, osend[0])

    def o_take(k):
        d = mixed_late(k, nz)
        source = lax.rem(z + d, nz)
        for q in range(len(OUT_CUTS) - 1):
            o_copy(q, d, source).wait()
        put(source, orecv[source])

    each(nz - 1, o_take)


def on_device(sizes, momentum, spectral_sq):
    nx, ny, nz, _ = sizes
    nb = 2 * nx
    nd = nb // 2 + 1
    rows, width = momentum.shape[1:]
    assert momentum.shape[0] == nz and width == nb * LANES and rows == ROWS
    part = LANES // ny
    short = ROWS * LANES
    nq = len(OUT_CUTS) - 1
    sem = pltpu.SemaphoreType.DMA
    vmem = pltpu.VMEM
    out = pl.pallas_call(
        lambda *refs: kernel(sizes, *refs),
        out_shape=jax.ShapeDtypeStruct((nz, 8, width), bf16),
        in_specs=[
            pl.BlockSpec(memory_space=pltpu.HBM),
            pl.BlockSpec(memory_space=pltpu.SMEM),
        ],
        out_specs=pl.BlockSpec(memory_space=pltpu.VMEM),
        scratch_shapes=[
            vmem((rows, nz, width), f32),
            vmem((nz, 8, short), bf16),
            vmem((2, nz, 8, short), bf16),
            vmem((2 * nz * 8, width), f32),
            vmem((2 * nz * 8, width), bf16),
            vmem((nd, nx, LANES, LANES), bf16),
            vmem((nd, nx, LANES, LANES), bf16),
            vmem((nd, LANES, LANES), f32),
            vmem((nd, ny, part, LANES), f32),
            vmem((nd, ny, part, LANES), bf16),
            vmem((nd, ny, part, LANES), bf16),
            vmem((nd, nb, ny, part, LANES), bf16),
            vmem((width, width), bf16),
            vmem((width, width), bf16),
            vmem((nz * 8, width), f32),
            vmem((nz * 8, short), f32),
            vmem((nz, 8, short), bf16),
            vmem((nz, 8, short), bf16),
            vmem((nx + 5, 8, LANES), f32),
            sem(()),
            sem((nz,)), sem((nz,)), sem((nz,)), sem((nz,)),
            sem((nd, nx)), sem((nd, nx)), sem((nd, ny)), sem((nd, ny)),
            sem((nd, ny)), sem((nd, ny)), sem((nd, nx)), sem((nd, nx)),
            sem((nd, nx)), sem((nd, nx)), sem((nq, nz)), sem((nq, nz)),
            sem((nx + 1,)), sem((nx + 1,)),
        ],
        compiler_params=pltpu.CompilerParams(
            collective_id=0, has_side_effects=True, vmem_limit_bytes=48 << 20
        ),
        name="muon_step",
    )(pltpu.with_memory_space_constraint(momentum.transpose(1, 0, 2), pltpu.HBM), spectral_sq)
    return out[:, :rows]


def solution(mesh):
    ne, nf = mesh.shape["expert"], mesh.shape["fsdp"]
    nx, nyl = ne // 4, 4
    nz = nf // nyl
    sizes = (nx, 2 * nyl, nz, nyl)
    finer = Mesh(mesh.devices.reshape(nx, 2, 2, nyl, nz), AXES)
    rows = P(None, ("yl", "z", "x", "yh", "core"), None)
    return jax.shard_map(
        lambda m, s: on_device(sizes, m, s),
        mesh=finer,
        in_specs=(rows, P(("x", "yh", "core"))),
        out_specs=rows,
        check_vma=False,
    )
```

time: 319 us -> 85.3 us (0.27)
  blocking collectives: 137 us -> 0 us
  waiting for transfers between devices: 122 us -> 0 us
  Pallas kernels: 0 us -> 83.6 us
  starting transfers between devices: 17.6 us -> 0 us
  local copies, waits for them, and re-layouts: 16.8 us -> 0.84 us
  between operations: 14.6 us -> 0.66 us
  other arithmetic: 3.66 us -> 0 us
  matrix products: 3.59 us -> 0 us
    reduce_scatter x2 -> x0, waiting for transfers between devices: 109 us -> none  [own_block(): blocks = lax.psum_scatter(blocks, axes[k], scatter_dimension=0, tiled=True)]
    pallas_call x0 -> x1, Pallas kernels: none -> 83.6 us  [on_device(): pl.pallas_call(lambda *refs: kernel(sizes, *refs), out_shape=jax.ShapeDty...]
    unnamed x2 -> x0, blocking collectives: 52.4 us -> none
    all_to_all x1 -> x0, blocking collectives: 46.4 us -> none  [on_device(): lax.all_to_all(result, 'expert', split_axis=1, concat_axis=0, tiled=True)]
    all_gather x3 -> x0, blocking collectives: 38.4 us -> none  [stacked_from(): blocks = lax.all_gather(blocks, axes[k])]
    all_to_all x1 -> x0, starting transfers between devices: 17.5 us -> none  [on_device(): lax.all_to_all(momentum, 'expert', split_axis=0, concat_axis=1, tiled=True)]
    all_to_all x1 -> x0, waiting for transfers between devices: 12.9 us -> none  [on_device(): lax.all_to_all(momentum, 'expert', split_axis=0, concat_axis=1, tiled=True)]
    unnamed x9 -> x0, local copies, waits for them, and re-layouts: 6.01 us -> none
  transfers between devices with their start and end apart: 4 -> 0, of which waited for: 3 -> 0; matrix products, arithmetic and copies ran while one was open for 3% -> 0% of each run, Pallas kernels for 0% -> 0%
where the time goes in v2:
time: 85.3 us; the launch traced here: 85.1 us
  Pallas kernels  83.6 us (98%)
    pallas_call x1, Pallas kernels, on_device(): pl.pallas_call(lambda *refs: kernel(sizes, *refs), out_shape=jax.ShapeDty...  83.6 us

profile of v2, /device:TPU:1, one launch (start us, length us, event | category | flops | bytes accessed | tf_op | source)
XLA Modules:
  0.0 85.1 jit_solution(8495171495291371585)
XLA Ops:
  0.7 83.6 %muon_step.1 = bf16[16,8,1024]{2,1,0:T(8,128)(2,1)S(1)} custom-call(f32[7,16,1024]{2,1,0:T(8,128)} %bitcast.3, f32[1]{0:T(128)S(6)} %copy.4.refs_1_), custom_call_target="tpu_custom_call" | custom-call | tf_op jit(solution)/shard_map/muon_step/pallas_call | solution.py:411
  84.3 0.8 copy.3

commit v3 on v2

--- a/solution.py
+++ b/solution.py
@@ -20,7 +20,8 @@
 
 CHUNKS = (1, 2, 3, 4, 0)
 STEPS = (
-    "X0 X1 X2 Y0 X3 Y1 X4 Y2 A0 Y3 A1 Y4 A2 B0 A3 B1 A4 B2 B3 B4".split()
+    "X0", "X1", "X2", "Y0", "X3", "Y1", "X4", "Y2", "A0", "Y3",
+    "A1", "Y4", "A2", "B0", "A3", "B1", "A4", "B2", "B3", "B4",
 )
 OUT_CUTS = (0, 384, 896)
 
@@ -158,14 +159,21 @@
         unpack(0, d)
 
     unpack(0, 0)
-    each(nz - 1, z_take)
 
     def swap_take(d):
         swap_copy(d).wait_recv()
         unpack(1, d)
 
+    lag = min(4, nz - 1)
+    each(lag, z_take)
     swap_take(0)
-    each(nz - 1, lambda k: swap_take(mixed_late(k, nz)))
+
+    def both(k):
+        z_take(k + lag)
+        swap_take(mixed_late(k, nz))
+
+    each(nz - 1 - lag, both)
+    each(lag, lambda k: swap_take(mixed_late(k + nz - 1 - lag, nz)))
     sq_core.wait_recv()
     sq[2] = sq[0] + sq[1]
 
@@ -344,7 +352,7 @@
     root = jnp.sqrt(f32(C)) / jnp.sqrt(sq[nx + 4])
 
     def tail_rows(d):
-        rows = pl.ds(pl.multiple_of(d * 8, 8), 8)
+        rows = pl.ds(d * 8, 8)
         tail[rows, :] = spread_rows(zrow[rows, short:] * root)
 
     def o_copy(q, d, source):
@@ -366,7 +374,8 @@
         cut = slice(OUT_CUTS[q], OUT_CUTS[q + 1])
         if q == 0:
             update_columns(slice(short, width), cut)
-            each(nz, tail_rows)
+            for d in range(nz):
+                tail_rows(d)
         else:
             update_columns(cut)
 

time: 85.3 us -> 85.1 us (level)
  no operation moved by 1% of the time
where the time goes in v3:
time: 85.1 us; the launch traced here: 84.9 us
  Pallas kernels  83.4 us (98%)
    pallas_call x1, Pallas kernels, on_device(): pl.pallas_call(lambda *refs: kernel(sizes, *refs), out_shape=jax.ShapeDty...  83.4 us

profile of v3, /device:TPU:1, one launch (start us, length us, event | category | flops | bytes accessed | tf_op | source)
XLA Modules:
  0.0 84.9 jit_solution(13353808687675604936)
XLA Ops:
  0.7 83.4 %muon_step.1 = bf16[16,8,1024]{2,1,0:T(8,128)(2,1)S(1)} custom-call(f32[7,16,1024]{2,1,0:T(8,128)} %bitcast.3, f32[1]{0:T(128)S(6)} %copy.4.refs_1_), custom_call_target="tpu_custom_call" | custom-call | tf_op jit(solution)/shard_map/muon_step/pallas_call | solution.py:420
  84.1 0.8 copy.3
